TPU v7x, 32 devices: a whole 2x2x4 slice. The times are simulated.
32 devices in a mesh: lat: 4 (over y, x), lon: 8 (over z, core).
Axes of the slice: x: 2, y: 2, z: 4, core: 2. Of those that a mesh axis runs over, the one named last changes fastest.
Arguments:
- fields: bfloat16 [192, 256, 2, 256], P('lat', 'lon'), may hold values from -6 to 6
- ocean_mask: int32 [24, 32], P('lat'), may hold values from 0 to 1, as said below
- gain_one: float32 [256], replicated, may hold values from 0.1 to 1.9
- w_qkv: bfloat16 [256, 768], replicated, may hold values from -0.375 to 0.375
- rel_bias: float32 [8, 675], replicated, may hold values from -80 to 150
- w_proj: bfloat16 [256, 256], replicated, may hold values from -0.375 to 0.375
- gain_two: float32 [256], replicated, may hold values from 0.1 to 1.9
- w_up: bfloat16 [256, 1024], replicated, may hold values from -0.375 to 0.375
- w_down: bfloat16 [1024, 256], replicated, may hold values from -0.1875 to 0.1875
Outputs:
- ocean_out: bfloat16 [192, 256, 2, 256], P('lat', 'lon')
Inputs may be any that keep to these rules, and one draw needn't show every extreme that they name: `ocean_mask`: the windows of the last row of windows (a = 23) are land. Each band of 6 rows of windows held by one index of lat holds exactly 10 ocean windows per longitude device. Taking the devices of a band in order of longitude index, each holding 4 columns of windows, the ocean windows of the first d devices number at least d * 10 and at most d * 10 + 10; the upper bound is reached for some d in every band, at places drawn anew. One device holds 0 to 20 ocean windows.
All inputs are finite; a program needn't handle non-finite values.
Results may differ from a plain program's by a relative error of at most 0.0057.
Values may be sent and summed in bfloat16 or wider, within the bound.
A program may use at most 64 MiB of HBM per device.

v0:
```python
import functools
import math

import jax
import jax.numpy as jnp
from jax import lax
from jax.experimental import pallas as pl
from jax.experimental.pallas import tpu as pltpu
from jax.sharding import PartitionSpec as P

WIN_LAT = 8
WIN_LON = 8
NORM_FLOOR = 0.25
MESH = pl.DeviceIdType.MESH
LOG2E = math.log2(math.e)
ROOT_HALF = math.sqrt(0.5)
PAIR = 2
EARLY_PAIRS = 2
LEAVING_PAIRS = 4


def dot(left, right):
    return jnp.dot(left, right, preferred_element_type=jnp.float32)


def normalise(values, gain):
    share = 1.0 / values.shape[0]
    average = jnp.sum(values, axis=0, keepdims=True) * share
    centred = values - average
    spread = jnp.sum(centred * centred, axis=0, keepdims=True) * share
    return (centred * lax.rsqrt(spread + NORM_FLOOR) * gain).astype(jnp.bfloat16)


def wide(gain, columns):
    return jnp.concatenate([gain] * (columns // gain.shape[1]), axis=1)


def attention_steps(store, blocks, weights):
    qkv_t, proj_t, gain, bias = weights["qkv"], weights["proj"], weights["gain_one"], weights["bias"]
    tokens, features = blocks[0].shape
    half = bias.shape[0]
    dim = features // (2 * half)
    scale = LOG2E / math.sqrt(dim)
    values = jnp.concatenate([block.T for block in blocks], axis=1).astype(jnp.float32)
    normed = normalise(values, wide(gain[...], values.shape[1]))
    yield
    key_t = dot(qkv_t[features : 2 * features], normed).astype(jnp.bfloat16)
    query_t = (dot(qkv_t[:features], normed) * scale).astype(jnp.bfloat16)
    value_t = dot(qkv_t[2 * features :], normed).astype(jnp.bfloat16)
    yield
    lane_head = lax.broadcasted_iota(jnp.int32, (tokens, features), 1) // dim % half
    nothing = jnp.zeros((features // 2, tokens), jnp.bfloat16)
    ones = jnp.ones((16, tokens), jnp.bfloat16)
    mixed = []
    for n in range(len(blocks)):
        lanes = slice(n * tokens, (n + 1) * tokens)
        key = key_t[:, lanes].T
        masked = [jnp.where(lane_head == h, key, jnp.zeros_like(key)) for h in range(half)]
        upper = jnp.concatenate([query_t[: features // 2, lanes], nothing], axis=1)
        lower = jnp.concatenate([nothing, query_t[features // 2 :, lanes]], axis=1)
        every = dot(jnp.concatenate(masked, axis=0), jnp.concatenate([upper, lower], axis=0))
        first, second = [], []
        for h in range(half):
            scores = every[h * tokens : (h + 1) * tokens] + bias[h]
            power = jnp.exp2(scores - jnp.max(scores, axis=0, keepdims=True)).astype(jnp.bfloat16)
            one, two = h * dim, (h + half) * dim
            rows = [value_t[one : one + dim, lanes], value_t[two : two + dim, lanes], ones]
            piece = dot(jnp.concatenate(rows, axis=0), power)
            share = 1.0 / piece[2 * dim : 2 * dim + 1]
            first.append((piece[:dim, :tokens] * share[:, :tokens]).astype(jnp.bfloat16))
            second.append((piece[dim : 2 * dim, tokens:] * share[:, tokens:]).astype(jnp.bfloat16))
            yield
        mixed.append(jnp.concatenate(first + second, axis=0))
    mixed_t = jnp.concatenate(mixed, axis=1)
    store.append((values + dot(proj_t[...], mixed_t)).astype(jnp.bfloat16))
    yield


def mlp_steps(store, middle, weights, tokens):
    up_t, down_t, gain = weights["up"], weights["down"], weights["gain_two"]
    features, hidden = middle.shape[0], up_t.shape[0]
    residual = middle.astype(jnp.float32)
    normed = normalise(residual, wide(gain[...], middle.shape[1]))
    yield
    total = None
    for part in range(hidden // features):
        rows = slice(part * features, (part + 1) * features)
        grown = dot(up_t[rows], normed).astype(jnp.bfloat16)
        yield
        grown = grown * (jnp.bfloat16(1.0) + lax.erf(grown))
        piece = dot(down_t[:, rows], grown)
        total = piece if total is None else total + piece
        yield
    result = (residual + total * ROOT_HALF).astype(jnp.bfloat16)
    for n in range(middle.shape[1] // tokens):
        store.append(result[:, n * tokens : (n + 1) * tokens].T)
    yield


def drain(*steps):
    for step in steps:
        for _ in step:
            pass


def attend(blocks, weights):
    store = []
    drain(attention_steps(store, blocks, weights))
    return store[0]


def expand(middle, weights, tokens):
    store = []
    drain(mlp_steps(store, middle, weights, tokens))
    return store


def both(blocks, middle, weights, tokens):
    new, finished = [], []
    drain(mlp_steps(finished, middle, weights, tokens), attention_steps(new, blocks, weights))
    return new[0], finished


def bias_strips(rel_bias, padded, strips, levels):
    heads, length = rel_bias.shape
    col_step = 2 * levels - 1
    row_step = (2 * WIN_LON - 1) * col_step
    offsets = [c * col_step + lev for c in range(WIN_LON) for lev in range(levels)]
    top = offsets[-1]
    width = padded.shape[1] - 128
    padded[...] = jnp.zeros_like(padded)
    padded[:, :length] = rel_bias[...] * LOG2E
    table = padded[...]
    left = jnp.concatenate([table[:, top - q : top - q + width] for q in offsets], axis=0)
    group = WIN_LON * levels
    lane = lax.broadcasted_iota(jnp.int32, (width, strips.shape[2]), 1)
    inner = lane % group
    target = lane // group * row_step + inner // levels * col_step + inner % levels
    pick = lax.broadcasted_iota(jnp.int32, target.shape, 0) == target
    found = jnp.dot(
        left,
        pick.astype(jnp.float32),
        precision=lax.Precision.HIGHEST,
        preferred_element_type=jnp.float32,
    )
    for place in range(group):
        strips[:, place, :] = found[place * heads : (place + 1) * heads]


def bias_table(strips, bias):
    heads, group, _ = strips.shape
    tokens = WIN_LAT * group
    for row in range(WIN_LAT):
        first = (WIN_LAT - 1 - row) * group
        piece = strips[:, :, first : first + tokens]
        places = slice(row * group, (row + 1) * group)
        bias[:, places, :tokens] = piece[: heads // 2]
        bias[:, places, tokens:] = piece[heads // 2 :]


class Sizes:
    def __init__(self, fields_shape):
        self.rows = fields_shape[0] // WIN_LAT
        self.cols = fields_shape[1] // WIN_LON
        self.count = self.rows * self.cols
        self.late = -(-((self.rows - 1) * self.cols // 2) // PAIR) * PAIR
        self.early = EARLY_PAIRS * PAIR
        self.leaving = min(LEAVING_PAIRS * PAIR, self.late)
        self.edge = self.rows + self.cols - 1

    def interior(self, window):
        return window // self.cols < self.rows - 1 and window % self.cols < self.cols - 1


def share_out(sizes, mask, device):
    def tally(d):
        inside, outside = jnp.int32(0), jnp.int32(0)
        for window in range(sizes.count):
            ocean = mask[window // sizes.cols, d * sizes.cols + window % sizes.cols]
            if sizes.interior(window):
                inside = inside + ocean
            else:
                outside = outside + ocean
        return inside, outside

    last = lax.axis_size("lon") - 1

    def pass_on(d, carried):
        inside, outside = tally(d)
        early = jnp.minimum(inside, sizes.early)
        excess = carried + inside + outside - early - sizes.late
        leaving = jnp.minimum(jnp.minimum(excess, inside - early), sizes.leaving)
        return jnp.where(d == last, 0, jnp.maximum(leaving, 0))

    coming = lax.fori_loop(0, device, pass_on, jnp.int32(0))
    leaving = pass_on(device, coming)
    inside, outside = tally(device)
    return coming, leaving, jnp.minimum(inside, sizes.early), inside, outside


def main_kernel(
    sizes,
    fields, mask, rel_bias, gain_one, w_qkv, w_proj, gain_two, w_up, w_down,
    finished, returned, ext, qkv_t, proj_t, up_t, down_t, gain_one_t, gain_two_t, bias,
    local, arrived, leave, middle, places, inner, outer, rel_local, padded, strips,
    gain_one_raw, gain_two_raw, qkv_raw, proj_raw, up_raw, down_raw,
    load_sems, halo_send, halo_recv, out_send, out_recv, back_send, back_recv,
):
    lat_cells, lon_cells, levels, features = fields.shape
    lat_half, lon_half = WIN_LAT // 2, WIN_LON // 2
    tokens = WIN_LAT * WIN_LON * levels
    lat, lon = lax.axis_index("lat"), lax.axis_index("lon")
    lat_size, lon_size = lax.axis_size("lat"), lax.axis_size("lon")
    last = lon_size - 1
    west, east = (lon + lon_size - 1) % lon_size, (lon + 1) % lon_size
    barrier = pltpu.get_barrier_semaphore()

    def greet(row, col):
        pl.semaphore_signal(barrier, inc=1, device_id=(row, col), device_id_type=MESH)

    greet(lat, east)
    greet(lat, west)

    @pl.when(lat < lat_size - 1)
    def _():
        greet(lat + 1, lon)
        greet(lat + 1, east)

    def load(which, source, target):
        copy = pltpu.make_async_copy(source, target, load_sems.at[which])
        copy.start()
        return copy

    here = load(0, fields, local)
    plan = load(1, mask, places)
    table = load(2, rel_bias, rel_local)
    inside = load(3, fields, ext.at[pl.ds(0, lat_cells), pl.ds(0, lon_cells)])
    raw = [gain_one_raw, gain_two_raw, qkv_raw, proj_raw, up_raw, down_raw]
    sources = [gain_one, gain_two, w_qkv, w_proj, w_up, w_down]
    weight_loads = [load(4 + n, source, target) for n, (source, target) in enumerate(zip(sources, raw))]

    def transfer(source, target, send, recv, row, col):
        return pltpu.make_async_remote_copy(
            src_ref=source, dst_ref=target, send_sem=send, recv_sem=recv,
            device_id=(row, col), device_id_type=MESH,
        )

    up = jnp.maximum(lat - 1, 0)
    below, beside = pl.ds(lat_cells, lat_half), pl.ds(lon_cells, lon_half)
    rows, cols = pl.ds(lat_half, lat_cells - lat_half), pl.ds(lon_half, lon_cells - lon_half)
    top, left = pl.ds(0, lat_half), pl.ds(0, lon_half)
    to_north = transfer(
        local.at[top, cols], ext.at[below, cols], halo_send.at[0], halo_recv.at[0], up, lon
    )
    to_west = transfer(
        local.at[rows, left], ext.at[rows, beside], halo_send.at[1], halo_recv.at[1], lat, west
    )
    to_corner = transfer(
        local.at[top, left], ext.at[below, beside], halo_send.at[2], halo_recv.at[2], up, west
    )

    plan.wait()
    coming, going, early, _, edges = share_out(sizes, places, lon)
    first_col = lon * sizes.cols
    for chain, inside_only in ((inner, True), (outer, False)):
        following = jnp.int32(sizes.count)
        chain[0, sizes.count] = following
        chain[0, sizes.count + 1] = following
        for window in reversed(range(sizes.count)):
            if sizes.interior(window) == inside_only:
                ocean = places[window // sizes.cols, first_col + window % sizes.cols]
                following = jnp.where(ocean == 1, window, following)
            chain[0, window] = following
        spot = following
        for n in range(sizes.count):
            chain[1, n] = jnp.where(spot == sizes.count, 0, spot)
            spot = chain[0, spot + 1]

    here.wait()

    @pl.when(lat > 0)
    def _():
        pl.semaphore_wait(barrier, 4)
        to_north.start()
        to_corner.start()

    @pl.when(lat == 0)
    def _():
        pl.semaphore_wait(barrier, 2)

    to_west.start()

    def fetch(source, window):
        row, col = window // sizes.cols, window % sizes.cols
        row_cells = pl.ds(row * WIN_LAT + lat_half, WIN_LAT)
        return source[row_cells, pl.ds(col * WIN_LON + lon_half, WIN_LON)]

    def outward(slot):
        return transfer(
            leave.at[slot], arrived.at[slot], out_send.at[slot], out_recv.at[slot],
            lat, jnp.minimum(lon + 1, last),
        )

    def homeward(pair):
        slots = pl.ds(pair * PAIR, PAIR)
        return transfer(
            finished.at[pl.ds(sizes.early + pair * PAIR, PAIR)], returned.at[slots],
            back_send.at[pair], back_recv.at[pair], lat, jnp.maximum(lon - 1, 0),
        )

    def pack(slot, carry):
        leave[slot] = fetch(local, inner[1, sizes.early + slot])

        @pl.when(lon < last)
        def _():
            outward(slot).start()

        return carry

    lax.fori_loop(0, sizes.leaving, pack, 0)

    table.wait()
    bias_strips(rel_local, padded, strips, levels)
    bias_table(strips, bias)
    for copy in weight_loads:
        copy.wait()
    gain_one_t[...] = jnp.broadcast_to(gain_one_raw[...], (128, features)).T
    gain_two_t[...] = jnp.broadcast_to(gain_two_raw[...] * ROOT_HALF, (128, features)).T
    for source, target in ((qkv_raw, qkv_t), (proj_raw, proj_t), (up_raw, up_t), (down_raw, down_t)):
        target[...] = source[...].T
    weights = dict(
        qkv=qkv_t, proj=proj_t, up=up_t, down=down_t,
        gain_one=gain_one_t, gain_two=gain_two_t, bias=bias,
    )
    early_pairs, late_pairs, leaving_pairs = (
        sizes.early // PAIR, sizes.late // PAIR, sizes.leaving // PAIR
    )

    def early_blocks(step):
        windows = [fetch(local, inner[1, step * PAIR + n]) for n in range(PAIR)]
        return [window.reshape(tokens, features) for window in windows]

    def late_blocks(pair):
        blocks = []
        for n in range(PAIR):
            slot = pair * PAIR + n
            rank = slot - coming
            edge = jnp.clip(rank, 0, sizes.count - 1)
            other = jnp.clip(early + going + rank - edges, 0, sizes.count - 1)
            mine = fetch(ext, jnp.where(rank < edges, outer[1, edge], inner[1, other]))
            sent = arrived[jnp.minimum(slot, sizes.leaving - 1)]
            block = jnp.where(rank >= 0, mine, sent)
            blocks.append(block.reshape(tokens, features))
        return blocks

    def keep(step, results):
        for n, result in enumerate(results):
            finished[step * PAIR + n] = result.reshape(finished.shape[1:])

    middle[0] = attend(early_blocks(0), weights)

    def early_step(step, carry):
        old = middle[(step + 1) % 2]
        new, results = both(early_blocks(step), old, weights, tokens)
        keep(step - 1, results)
        middle[step % 2] = new
        return carry

    lax.fori_loop(1, early_pairs, early_step, 0)
    inside.wait()
    to_west.wait_recv()

    @pl.when(lat < lat_size - 1)
    def _():
        to_north.wait_recv()
        to_corner.wait_recv()

    def send_home(pair):
        @pl.when((pair >= 0) & (pair < leaving_pairs) & (lon > 0))
        def _():
            homeward(pair).start()

    def late_step(pair, carry):
        @pl.when((pair < leaving_pairs) & (lon > 0))
        def _():
            for n in range(PAIR):
                outward(pair * PAIR + n).wait_recv()

        step = early_pairs + pair
        old = middle[(step + 1) % 2]
        new, results = both(late_blocks(pair), old, weights, tokens)
        keep(step - 1, results)
        middle[step % 2] = new
        send_home(pair - 1)
        return carry

    lax.fori_loop(0, late_pairs, late_step, 0)
    steps = early_pairs + late_pairs
    keep(steps - 1, expand(middle[(steps - 1) % 2], weights, tokens))
    if late_pairs <= leaving_pairs:
        send_home(jnp.int32(late_pairs - 1))

    to_west.wait_send()

    @pl.when(lat > 0)
    def _():
        to_north.wait_send()
        to_corner.wait_send()

    @pl.when(lon > 0)
    def _():
        for pair in range(leaving_pairs):
            homeward(pair).wait_send()

    @pl.when(lon < last)
    def _():
        for slot in range(sizes.leaving):
            outward(slot).wait_send()
        for pair in range(leaving_pairs):
            homeward(pair).wait_recv()


def place_kernel(
    sizes,
    mask, where, finished, returned, ext, qkv_t, proj_t, up_t, down_t, gain_one_t, gain_two_t, bias,
    result, zero, extra, sems,
):
    lat_half, lon_half = WIN_LAT // 2, WIN_LON // 2
    coming, going, early, _, edges = share_out(sizes, mask, where[0])
    first_col = where[0] * sizes.cols
    room = sizes.late - coming
    zero[...] = jnp.zeros_like(zero)

    def spot(window):
        row, col = window // sizes.cols, window % sizes.cols
        return result.at[pl.ds(row * WIN_LAT, WIN_LAT), pl.ds(col * WIN_LON, WIN_LON)]

    def send(source, window):
        pltpu.make_async_copy(source, spot(window), sems.at[window]).start()

    def visit(leftover, window, carry):
        inside_rank, edge_rank = carry
        row, col = window // sizes.cols, window % sizes.cols
        ocean = mask[row, first_col + col]
        edge = ((row == sizes.rows - 1) | (col == sizes.cols - 1)).astype(jnp.int32)
        rank = jnp.where(edge == 1, edge_rank, edges + inside_rank - early - going)
        is_early = (edge == 0) & (inside_rank < early)
        is_gone = (edge == 0) & (inside_rank >= early) & (inside_rank < early + going)
        rest = (ocean == 1) & jnp.logical_not(is_early | is_gone)
        if leftover:

            @pl.when(rest & (rank >= room))
            def _():
                row_cells = pl.ds(row * WIN_LAT + lat_half, WIN_LAT)
                block = ext[row_cells, pl.ds(col * WIN_LON + lon_half, WIN_LON)]
                weights = dict(
                    qkv=qkv_t, proj=proj_t, up=up_t, down=down_t,
                    gain_one=gain_one_t, gain_two=gain_two_t, bias=bias,
                )
                tokens = block.shape[0] * block.shape[1] * block.shape[2]
                middle = attend([block.reshape(tokens, block.shape[3])], weights)
                extra[...] = expand(middle, weights, tokens)[0].reshape(extra.shape)
                copy = pltpu.make_async_copy(extra, spot(window), sems.at[window])
                copy.start()
                copy.wait()

        else:

            @pl.when(ocean == 0)
            def _():
                send(zero, window)

            @pl.when((ocean == 1) & is_early)
            def _():
                send(finished.at[inside_rank], window)

            @pl.when((ocean == 1) & is_gone)
            def _():
                send(returned.at[inside_rank - early], window)

            @pl.when(rest & (rank < room))
            def _():
                send(finished.at[sizes.early + coming + rank], window)

        mine = ocean * (1 - edge)
        left = jnp.where(rest & (rank >= room), 1, 0)
        return inside_rank + mine, edge_rank + ocean * edge, left

    def start(window, carry):
        inside_rank, edge_rank, total, lost = carry
        inside_rank, edge_rank, left = visit(False, window, (inside_rank, edge_rank))
        return inside_rank, edge_rank, total + left, lost | (left << window)

    none = jnp.int32(0)
    _, _, total, lost = lax.fori_loop(0, sizes.count, start, (none, none, none, none))

    @pl.when(total > 0)
    def _():
        def again(window, carry):
            inside_rank, edge_rank, _ = visit(True, window, carry)
            return inside_rank, edge_rank

        lax.fori_loop(0, sizes.count, again, (none, none))

    def finish(window, carry):
        @pl.when((lost >> window) & 1 == 0)
        def _():
            pltpu.make_async_copy(zero, spot(window), sems.at[window]).wait()

        return carry

    lax.fori_loop(0, sizes.count, finish, 0)


def vmem():
    return pl.BlockSpec(memory_space=pltpu.VMEM)


def smem():
    return pl.BlockSpec(memory_space=pltpu.SMEM)


def any_space():
    return pl.BlockSpec(memory_space=pl.ANY)


def cost(flops, moved):
    return pl.CostEstimate(flops=flops, bytes_accessed=moved, transcendentals=0)


def body(fields, ocean_mask, gain_one, w_qkv, rel_bias, w_proj, gain_two, w_up, w_down):
    sizes = Sizes(fields.shape)
    lat_cells, lon_cells, levels, features = fields.shape
    heads, length = rel_bias.shape
    group = WIN_LON * levels
    tokens = WIN_LAT * group
    window = (WIN_LAT, WIN_LON, levels, features)
    bf16, f32 = jnp.bfloat16, jnp.float32
    shape = jax.ShapeDtypeStruct
    gains = [gain_one.reshape(1, -1), gain_two.reshape(1, -1)]
    sources = [w_qkv, w_proj, w_up, w_down]
    flips = [shape(w.shape[::-1], w.dtype) for w in sources]
    dma = pltpu.SemaphoreType.DMA
    pairs = sizes.leaving // PAIR
    results = pl.pallas_call(
        functools.partial(main_kernel, sizes),
        out_shape=[
            shape((sizes.early + sizes.late,) + window, bf16),
            shape((sizes.leaving,) + window, bf16),
            shape((lat_cells + WIN_LAT // 2, lon_cells + WIN_LON // 2, levels, features), bf16),
        ]
        + flips
        + [shape((features, 128), f32)] * 2
        + [shape((heads // 2, tokens, 2 * tokens), f32)],
        in_specs=[any_space()] * 9,
        out_specs=[vmem()] * 10,
        scratch_shapes=[
            pltpu.VMEM(fields.shape, bf16),
            pltpu.VMEM((sizes.leaving,) + window, bf16),
            pltpu.VMEM((sizes.leaving,) + window, bf16),
            pltpu.VMEM((2, features, PAIR * tokens), bf16),
            pltpu.SMEM(ocean_mask.shape, jnp.int32),
            pltpu.SMEM((2, sizes.count + 2), jnp.int32),
            pltpu.SMEM((2, sizes.count + 2), jnp.int32),
            pltpu.VMEM(rel_bias.shape, f32),
            pltpu.VMEM((heads, (length + 255) // 128 * 128), f32),
            pltpu.VMEM((heads, group, 2 * tokens), f32),
        ]
        + [pltpu.VMEM(gain.shape, f32) for gain in gains]
        + [pltpu.VMEM(w.shape, bf16) for w in sources]
        + [dma((10,)), dma((3,)), dma((3,)), dma((sizes.leaving,)), dma((sizes.leaving,))]
        + [dma((pairs,)), dma((pairs,))],
        cost_estimate=cost(0, fields.size),
        compiler_params=pltpu.CompilerParams(
            collective_id=0, has_side_effects=True, vmem_limit_bytes=40 * 2**20
        ),
    )(fields, ocean_mask, rel_bias, gains[0], w_qkv, w_proj, gains[1], w_up, w_down)
    where = jnp.reshape(lax.axis_index("lon"), (1,)).astype(jnp.int32)
    return pl.pallas_call(
        functools.partial(place_kernel, sizes),
        out_shape=shape(fields.shape, fields.dtype),
        in_specs=[smem()] * 2 + [vmem()] * 10,
        out_specs=any_space(),
        scratch_shapes=[
            pltpu.VMEM(window, bf16),
            pltpu.VMEM(window, bf16),
            dma((sizes.count,)),
        ],
        cost_estimate=cost(0, 4 * fields.size),
        compiler_params=pltpu.CompilerParams(vmem_limit_bytes=12 * 2**20),
    )(ocean_mask, where, *results)


def solution(mesh):
    in_specs = (P("lat", "lon", None, None), P("lat", None), P(), P(), P(), P(), P(), P(), P())
    out_specs = P("lat", "lon", None, None)
    return jax.shard_map(body, mesh=mesh, in_specs=in_specs, out_specs=out_specs, check_vma=False)
```

profile of v0, /device:TPU:1, one launch (start us, length us, event | category | flops | bytes accessed | tf_op | source)
XLA Modules:
  0.0 30.5 jit_solution(15071597220835155301)
XLA Ops:
  0.0 0.0 copy-start
  0.0 1.4 %copy-done = bf16[48,32,2,256]{3,2,1,0:T(2,128)(2,1)S(1)} copy-done((bf16[48,32,2,256]{3,2,1,0:T(2,128)(2,1)S(1)}, bf16[48,32,2,256]{3,2,1,0:T(2,128)(2,1)}, u32[]{:S(2)}) %copy-start) | copy-done | bytes 1572888
  1.4 0.0 copy-start.1
  1.4 1.0 %copy-done.1 = bf16[256,1024]{1,0:T(8,128)(2,1)S(1)} copy-done((bf16[256,1024]{1,0:T(8,128)(2,1)S(1)}, bf16[256,1024]{1,0:T(8,128)(2,1)}, u32[]{:S(2)}) %copy-start.1) | copy-done | bytes 524312
  2.5 0.0 copy-start.2
  2.5 1.0 %copy-done.2 = bf16[1024,256]{1,0:T(8,128)(2,1)S(1)} copy-done((bf16[1024,256]{1,0:T(8,128)(2,1)S(1)}, bf16[1024,256]{1,0:T(8,128)(2,1)}, u32[]{:S(2)}) %copy-start.2) | copy-done | bytes 524312
  3.5 0.0 copy-start.3
  3.5 1.0 %copy-done.3 = bf16[256,768]{1,0:T(8,128)(2,1)S(1)} copy-done((bf16[256,768]{1,0:T(8,128)(2,1)S(1)}, bf16[256,768]{1,0:T(8,128)(2,1)}, u32[]{:S(2)}) %copy-start.3) | copy-done | bytes 393240
  4.5 0.0 copy-start.4
  4.5 0.9 %copy-done.4 = bf16[256,256]{1,0:T(8,128)(2,1)S(1)} copy-done((bf16[256,256]{1,0:T(8,128)(2,1)S(1)}, bf16[256,256]{1,0:T(8,128)(2,1)}, u32[]{:S(2)}) %copy-start.4) | copy-done | bytes 131096
  5.4 0.0 copy-start.5
  5.4 0.7 %copy-done.5 = f32[8,675]{1,0:T(8,128)S(1)} copy-done((f32[8,675]{1,0:T(8,128)S(1)}, f32[8,675]{1,0:T(8,128)}, u32[]{:S(2)}) %copy-start.5) | copy-done | bytes 21624
  6.1 0.0 copy-start.6
  6.1 0.7 %copy-done.6 = s32[6,32]{1,0:T(8,128)S(1)} copy-done((s32[6,32]{1,0:T(8,128)S(1)}, s32[6,32]{1,0:T(8,128)}, u32[]{:S(2)}) %copy-start.6) | copy-done | bytes 792
  6.8 0.0 copy-start.7
  6.8 0.7 %copy-done.7 = f32[256]{0:T(256)S(1)} copy-done((f32[256]{0:T(256)S(1)}, f32[256]{0:T(256)}, u32[]{:S(2)}) %copy-start.7) | copy-done | bytes 1048
  7.5 0.0 copy-start.8
  7.5 0.7 %copy-done.8 = f32[256]{0:T(256)S(1)} copy-done((f32[256]{0:T(256)S(1)}, f32[256]{0:T(256)}, u32[]{:S(2)}) %copy-start.8) | copy-done | bytes 1048
  8.2 20.0 %shard_map.91 = (bf16[14,8,8,2,256]{4,3,2,1,0:T(2,128)(2,1)S(1)}, bf16[8,8,8,2,256]{4,3,2,1,0:T(2,128)(2,1)S(1)}, bf16[52,36,2,256]{3,2,1,0:T(2,128)(2,1)S(1)}, ...) custom-call(bf16[48,32,2,256]{3,2,1,0:T(2,128)(2,1)S(1)} %copy-done,, ...), custom_call_target="tpu_custom_call" | custom-call | bytes 786432 | tf_op jit(solution)/shard_map/pallas_call | solution.py:545
  28.2 2.3 %shard_map.92 = bf16[48,32,2,256]{3,2,1,0:T(2,128)(2,1)} custom-call(s32[6,32]{1,0:T(8,128)S(1)} %copy-done.6, s32[1]{0:T(128)} %bitcast.where, bf16[14,8,8,2,256]{4,3,2,1,0:T(2,128)(2,1)S(1)} %get-tuple-element.15.finished, bf16[8,8,8,2,256]{4,3,2,1,0:T(2,128)(2,1)S(1)} %get-tuple-element.16.returned, bf16[52,36,2,256]{3,2,1,0:T(2,128)(2,1)S(1)} %get-tuple-element.17.ext, ...), custom_call_target="tpu_custom_call" | custom-call | bytes 3145728 | tf_op jit(solution)/shard_map/pallas_call | solution.py:579
Async XLA Ops:
  0.0 1.4 %copy-start = (bf16[48,32,2,256]{3,2,1,0:T(2,128)(2,1)S(1)}, bf16[48,32,2,256]{3,2,1,0:T(2,128)(2,1)}, u32[]{:S(2)}) copy-start(bf16[48,32,2,256]{3,2,1,0:T(2,128)(2,1)} %fields.1) | copy-start | bytes 4718596
  1.4 1.0 %copy-start.1 = (bf16[256,1024]{1,0:T(8,128)(2,1)S(1)}, bf16[256,1024]{1,0:T(8,128)(2,1)}, u32[]{:S(2)}) copy-start(bf16[256,1024]{1,0:T(8,128)(2,1)} %w_up.1) | copy-start | bytes 1572868
  2.5 1.0 %copy-start.2 = (bf16[1024,256]{1,0:T(8,128)(2,1)S(1)}, bf16[1024,256]{1,0:T(8,128)(2,1)}, u32[]{:S(2)}) copy-start(bf16[1024,256]{1,0:T(8,128)(2,1)} %w_down.1) | copy-start | bytes 1572868
  3.5 1.0 %copy-start.3 = (bf16[256,768]{1,0:T(8,128)(2,1)S(1)}, bf16[256,768]{1,0:T(8,128)(2,1)}, u32[]{:S(2)}) copy-start(bf16[256,768]{1,0:T(8,128)(2,1)} %w_qkv.1) | copy-start | bytes 1179652
  4.5 0.9 %copy-start.4 = (bf16[256,256]{1,0:T(8,128)(2,1)S(1)}, bf16[256,256]{1,0:T(8,128)(2,1)}, u32[]{:S(2)}) copy-start(bf16[256,256]{1,0:T(8,128)(2,1)} %w_proj.1) | copy-start | bytes 393220
  5.4 0.7 %copy-start.5 = (f32[8,675]{1,0:T(8,128)S(1)}, f32[8,675]{1,0:T(8,128)}, u32[]{:S(2)}) copy-start(f32[8,675]{1,0:T(8,128)} %rel_bias.1) | copy-start | bytes 64804
  6.1 0.7 %copy-start.6 = (s32[6,32]{1,0:T(8,128)S(1)}, s32[6,32]{1,0:T(8,128)}, u32[]{:S(2)}) copy-start(s32[6,32]{1,0:T(8,128)} %mask.3) | copy-start | bytes 2308
  6.8 0.7 %copy-start.7 = (f32[256]{0:T(256)S(1)}, f32[256]{0:T(256)}, u32[]{:S(2)}) copy-start(f32[256]{0:T(256)} %param.11) | copy-start | bytes 3076
  7.5 0.7 %copy-start.8 = (f32[256]{0:T(256)S(1)}, f32[256]{0:T(256)}, u32[]{:S(2)}) copy-start(f32[256]{0:T(256)} %param.15) | copy-start | bytes 3076
where the time goes:
time: 30.9 us; the launch traced here: 30.5 us
  Pallas kernels  22.3 us (72%)
  local copies, waits for them, and re-layouts  8.17 us (26%)
    pallas_call x1, Pallas kernels, body(): pl.pallas_call(functools.partial(main_kernel, sizes), out_shape=[shape((s...  20 us
    unnamed x18, local copies, waits for them, and re-layouts  8.17 us
    pallas_call x1, Pallas kernels, body(): pl.pallas_call(functools.partial(place_kernel, sizes), out_shape=shape(fi...  2.31 us

commit v1 on v0

--- a/solution.py
+++ b/solution.py
@@ -198,13 +198,31 @@
     return coming, leaving, jnp.minimum(inside, sizes.early), inside, outside
 
 
+HEAD = 4
+
+
+def plan_kernel(sizes, mask, where, plan):
+    device = where[0]
+    coming, going, early, _, edges = share_out(sizes, mask, device)
+    for n, value in enumerate((coming, going, early, edges)):
+        plan[n] = value
+    for n in range(HEAD, HEAD + 2 * sizes.count + 2):
+        plan[n] = 0
+    for base, inside_only in ((HEAD, True), (HEAD + sizes.count + 1, False)):
+        spot = jnp.int32(base)
+        for window in range(sizes.count):
+            if sizes.interior(window) == inside_only:
+                ocean = mask[window // sizes.cols, device * sizes.cols + window % sizes.cols]
+                plan[spot] = window * ocean
+                spot = spot + ocean
+
+
 def main_kernel(
     sizes,
-    fields, mask, rel_bias, gain_one, w_qkv, w_proj, gain_two, w_up, w_down,
+    plan, fields, rel_bias, gain_one, w_qkv, w_proj, gain_two, w_up, w_down,
     finished, returned, ext, qkv_t, proj_t, up_t, down_t, gain_one_t, gain_two_t, bias,
-    local, arrived, leave, middle, places, inner, outer, rel_local, padded, strips,
-    gain_one_raw, gain_two_raw, qkv_raw, proj_raw, up_raw, down_raw,
-    load_sems, halo_send, halo_recv, out_send, out_recv, back_send, back_recv,
+    arrived, leave, middle, padded, strips,
+    halo_send, halo_recv, out_send, out_recv, back_send, back_recv,
 ):
     lat_cells, lon_cells, levels, features = fields.shape
     lat_half, lon_half = WIN_LAT // 2, WIN_LON // 2
@@ -226,18 +244,13 @@
         greet(lat + 1, lon)
         greet(lat + 1, east)
 
-    def load(which, source, target):
-        copy = pltpu.make_async_copy(source, target, load_sems.at[which])
-        copy.start()
-        return copy
-
-    here = load(0, fields, local)
-    plan = load(1, mask, places)
-    table = load(2, rel_bias, rel_local)
-    inside = load(3, fields, ext.at[pl.ds(0, lat_cells), pl.ds(0, lon_cells)])
-    raw = [gain_one_raw, gain_two_raw, qkv_raw, proj_raw, up_raw, down_raw]
-    sources = [gain_one, gain_two, w_qkv, w_proj, w_up, w_down]
-    weight_loads = [load(4 + n, source, target) for n, (source, target) in enumerate(zip(sources, raw))]
+    coming, going, early, edges = (plan[n] for n in range(HEAD))
+
+    def inner(rank):
+        return plan[HEAD + rank]
+
+    def outer(rank):
+        return plan[HEAD + sizes.count + 1 + rank]
 
     def transfer(source, target, send, recv, row, col):
         return pltpu.make_async_remote_copy(
@@ -250,33 +263,14 @@
     rows, cols = pl.ds(lat_half, lat_cells - lat_half), pl.ds(lon_half, lon_cells - lon_half)
     top, left = pl.ds(0, lat_half), pl.ds(0, lon_half)
     to_north = transfer(
-        local.at[top, cols], ext.at[below, cols], halo_send.at[0], halo_recv.at[0], up, lon
+        fields.at[top, cols], ext.at[below, cols], halo_send.at[0], halo_recv.at[0], up, lon
     )
     to_west = transfer(
-        local.at[rows, left], ext.at[rows, beside], halo_send.at[1], halo_recv.at[1], lat, west
+        fields.at[rows, left], ext.at[rows, beside], halo_send.at[1], halo_recv.at[1], lat, west
     )
     to_corner = transfer(
-        local.at[top, left], ext.at[below, beside], halo_send.at[2], halo_recv.at[2], up, west
+        fields.at[top, left], ext.at[below, beside], halo_send.at[2], halo_recv.at[2], up, west
     )
-
-    plan.wait()
-    coming, going, early, _, edges = share_out(sizes, places, lon)
-    first_col = lon * sizes.cols
-    for chain, inside_only in ((inner, True), (outer, False)):
-        following = jnp.int32(sizes.count)
-        chain[0, sizes.count] = following
-        chain[0, sizes.count + 1] = following
-        for window in reversed(range(sizes.count)):
-            if sizes.interior(window) == inside_only:
-                ocean = places[window // sizes.cols, first_col + window % sizes.cols]
-                following = jnp.where(ocean == 1, window, following)
-            chain[0, window] = following
-        spot = following
-        for n in range(sizes.count):
-            chain[1, n] = jnp.where(spot == sizes.count, 0, spot)
-            spot = chain[0, spot + 1]
-
-    here.wait()
 
     @pl.when(lat > 0)
     def _():
@@ -309,7 +303,7 @@
         )
 
     def pack(slot, carry):
-        leave[slot] = fetch(local, inner[1, sizes.early + slot])
+        leave[slot] = fetch(fields, inner(sizes.early + slot))
 
         @pl.when(lon < last)
         def _():
@@ -318,15 +312,17 @@
         return carry
 
     lax.fori_loop(0, sizes.leaving, pack, 0)
-
-    table.wait()
-    bias_strips(rel_local, padded, strips, levels)
+    for row in range(lat_half, lat_cells, WIN_LAT):
+        cells = pl.ds(row, min(WIN_LAT, lat_cells - row))
+        ext[cells, pl.ds(lon_half, lon_cells - lon_half)] = fields[
+            cells, pl.ds(lon_half, lon_cells - lon_half)
+        ]
+
+    bias_strips(rel_bias, padded, strips, levels)
     bias_table(strips, bias)
-    for copy in weight_loads:
-        copy.wait()
-    gain_one_t[...] = jnp.broadcast_to(gain_one_raw[...], (128, features)).T
-    gain_two_t[...] = jnp.broadcast_to(gain_two_raw[...] * ROOT_HALF, (128, features)).T
-    for source, target in ((qkv_raw, qkv_t), (proj_raw, proj_t), (up_raw, up_t), (down_raw, down_t)):
+    gain_one_t[...] = jnp.broadcast_to(gain_one[...], (128, features)).T
+    gain_two_t[...] = jnp.broadcast_to(gain_two[...] * ROOT_HALF, (128, features)).T
+    for source, target in ((w_qkv, qkv_t), (w_proj, proj_t), (w_up, up_t), (w_down, down_t)):
         target[...] = source[...].T
     weights = dict(
         qkv=qkv_t, proj=proj_t, up=up_t, down=down_t,
@@ -337,7 +333,7 @@
     )
 
     def early_blocks(step):
-        windows = [fetch(local, inner[1, step * PAIR + n]) for n in range(PAIR)]
+        windows = [fetch(fields, inner(step * PAIR + n)) for n in range(PAIR)]
         return [window.reshape(tokens, features) for window in windows]
 
     def late_blocks(pair):
@@ -347,7 +343,7 @@
             rank = slot - coming
             edge = jnp.clip(rank, 0, sizes.count - 1)
             other = jnp.clip(early + going + rank - edges, 0, sizes.count - 1)
-            mine = fetch(ext, jnp.where(rank < edges, outer[1, edge], inner[1, other]))
+            mine = fetch(ext, jnp.where(rank < edges, outer(edge), inner(other)))
             sent = arrived[jnp.minimum(slot, sizes.leaving - 1)]
             block = jnp.where(rank >= 0, mine, sent)
             blocks.append(block.reshape(tokens, features))
@@ -367,7 +363,6 @@
         return carry
 
     lax.fori_loop(1, early_pairs, early_step, 0)
-    inside.wait()
     to_west.wait_recv()
 
     @pl.when(lat < lat_size - 1)
@@ -422,11 +417,11 @@
 
 def place_kernel(
     sizes,
-    mask, where, finished, returned, ext, qkv_t, proj_t, up_t, down_t, gain_one_t, gain_two_t, bias,
+    mask, where, plan, finished, returned, ext, qkv_t, proj_t, up_t, down_t, gain_one_t, gain_two_t, bias,
     result, zero, extra, sems,
 ):
     lat_half, lon_half = WIN_LAT // 2, WIN_LON // 2
-    coming, going, early, _, edges = share_out(sizes, mask, where[0])
+    coming, going, early, edges = (plan[n] for n in range(HEAD))
     first_col = where[0] * sizes.cols
     room = sizes.late - coming
     zero[...] = jnp.zeros_like(zero)
@@ -542,6 +537,15 @@
     flips = [shape(w.shape[::-1], w.dtype) for w in sources]
     dma = pltpu.SemaphoreType.DMA
     pairs = sizes.leaving // PAIR
+    where = jnp.reshape(lax.axis_index("lon"), (1,)).astype(jnp.int32)
+    plan = pl.pallas_call(
+        functools.partial(plan_kernel, sizes),
+        out_shape=shape((HEAD + 2 * sizes.count + 2,), jnp.int32),
+        in_specs=[smem()] * 2,
+        out_specs=smem(),
+        cost_estimate=cost(2**36, 2**26),
+        compiler_params=pltpu.CompilerParams(vmem_limit_bytes=2**20),
+    )(ocean_mask, where)
     results = pl.pallas_call(
         functools.partial(main_kernel, sizes),
         out_shape=[
@@ -552,34 +556,26 @@
         + flips
         + [shape((features, 128), f32)] * 2
         + [shape((heads // 2, tokens, 2 * tokens), f32)],
-        in_specs=[any_space()] * 9,
+        in_specs=[smem()] + [vmem()] * 8,
         out_specs=[vmem()] * 10,
         scratch_shapes=[
-            pltpu.VMEM(fields.shape, bf16),
             pltpu.VMEM((sizes.leaving,) + window, bf16),
             pltpu.VMEM((sizes.leaving,) + window, bf16),
             pltpu.VMEM((2, features, PAIR * tokens), bf16),
-            pltpu.SMEM(ocean_mask.shape, jnp.int32),
-            pltpu.SMEM((2, sizes.count + 2), jnp.int32),
-            pltpu.SMEM((2, sizes.count + 2), jnp.int32),
-            pltpu.VMEM(rel_bias.shape, f32),
             pltpu.VMEM((heads, (length + 255) // 128 * 128), f32),
             pltpu.VMEM((heads, group, 2 * tokens), f32),
         ]
-        + [pltpu.VMEM(gain.shape, f32) for gain in gains]
-        + [pltpu.VMEM(w.shape, bf16) for w in sources]
-        + [dma((10,)), dma((3,)), dma((3,)), dma((sizes.leaving,)), dma((sizes.leaving,))]
+        + [dma((3,)), dma((3,)), dma((sizes.leaving,)), dma((sizes.leaving,))]
         + [dma((pairs,)), dma((pairs,))],
         cost_estimate=cost(0, fields.size),
         compiler_params=pltpu.CompilerParams(
-            collective_id=0, has_side_effects=True, vmem_limit_bytes=40 * 2**20
+            collective_id=0, has_side_effects=True, vmem_limit_bytes=24 * 2**20
         ),
-    )(fields, ocean_mask, rel_bias, gains[0], w_qkv, w_proj, gains[1], w_up, w_down)
-    where = jnp.reshape(lax.axis_index("lon"), (1,)).astype(jnp.int32)
+    )(plan, fields, rel_bias, gains[0], w_qkv, w_proj, gains[1], w_up, w_down)
     return pl.pallas_call(
         functools.partial(place_kernel, sizes),
         out_shape=shape(fields.shape, fields.dtype),
-        in_specs=[smem()] * 2 + [vmem()] * 10,
+        in_specs=[smem()] * 3 + [vmem()] * 10,
         out_specs=any_space(),
         scratch_shapes=[
             pltpu.VMEM(window, bf16),
@@ -588,7 +584,7 @@
         ],
         cost_estimate=cost(0, 4 * fields.size),
         compiler_params=pltpu.CompilerParams(vmem_limit_bytes=12 * 2**20),
-    )(ocean_mask, where, *results)
+    )(ocean_mask, where, plan, *results)
 
 
 def solution(mesh):

time: 30.9 us -> 25.1 us (0.81)
  local copies, waits for them, and re-layouts: 8.17 us -> 1.15 us
  Pallas kernels: 22.3 us -> 23.7 us
    unnamed x18 -> x20, local copies, waits for them, and re-layouts: 8.17 us -> 1.15 us
    pallas_call x0 -> x1, Pallas kernels: none -> 1.34 us  [body(): pl.pallas_call(functools.partial(plan_kernel, sizes), out_shape=shape((HE...]
where the time goes in v1:
time: 25.1 us; the launch traced here: 24.9 us
  Pallas kernels  23.7 us (94%)
  local copies, waits for them, and re-layouts  1.15 us (5%)
    pallas_call x1, Pallas kernels, body(): pl.pallas_call(functools.partial(main_kernel, sizes), out_shape=[shape((s...  20.1 us
    pallas_call x1, Pallas kernels, body(): pl.pallas_call(functools.partial(place_kernel, sizes), out_shape=shape(fi...  2.25 us
    pallas_call x1, Pallas kernels, body(): pl.pallas_call(functools.partial(plan_kernel, sizes), out_shape=shape((HE...  1.34 us
    unnamed x20, local copies, waits for them, and re-layouts  1.15 us

profile of v1, /device:TPU:1, one launch (start us, length us, event | category | flops | bytes accessed | tf_op | source)
XLA Modules:
  0.0 24.9 jit_solution(2261698276354785631)
XLA Ops:
  0.0 0.0 copy-start.6
  0.0 0.7 %copy-done.6 = s32[6,32]{1,0:T(8,128)S(1)} copy-done((s32[6,32]{1,0:T(8,128)S(1)}, s32[6,32]{1,0:T(8,128)}, u32[]{:S(2)}) %copy-start.6) | copy-done | bytes 792
  0.7 0.0 copy-start
  0.7 0.0 copy-start.1
  0.7 0.0 copy-start.2
  0.7 0.0 copy-start.3
  0.7 0.0 copy-start.4
  0.7 0.0 copy-start.5
  0.7 0.0 copy-start.8
  0.7 0.0 copy-start.9
  0.7 1.3 %shard_map.91.plan = s32[54]{0:T(128)S(1)} custom-call(s32[6,32]{1,0:T(8,128)S(1)} %copy-done.6, s32[1]{0:T(128)} %bitcast.where), custom_call_target="tpu_custom_call" | custom-call | flops 68719476736 | bytes 67108864 | tf_op jit(solution)/shard_map/pallas_call | solution.py:541
  2.1 0.0 copy-done
  2.1 0.1 copy-done.1
  2.2 0.2 copy-done.2
  2.4 0.1 copy-done.3
  2.5 0.0 copy-done.4
  2.5 0.0 copy-done.5
  2.5 0.0 copy-done.8
  2.5 0.0 copy-done.9
  2.5 0.0 copy-start.7
  2.5 20.1 %shard_map.92 = (bf16[14,8,8,2,256]{4,3,2,1,0:T(2,128)(2,1)S(1)}, bf16[8,8,8,2,256]{4,3,2,1,0:T(2,128)(2,1)S(1)}, bf16[52,36,2,256]{3,2,1,0:T(2,128)(2,1)S(1)}, ...) custom-call(s32[54]{0:T(128)S(1)} %shard_map.91.plan, ...), custom_call_target="tpu_custom_call" | custom-call | bytes 786432 | tf_op jit(solution)/shard_map/pallas_call | solution.py:549
  22.7 0.0 copy-done.7
  22.7 2.2 %shard_map.93 = bf16[48,32,2,256]{3,2,1,0:T(2,128)(2,1)} custom-call(s32[6,32]{1,0:T(8,128)S(1)} %copy-done.7, s32[1]{0:T(128)} %bitcast.where, s32[54]{0:T(128)S(1)} %shard_map.91.plan, bf16[14,8,8,2,256]{4,3,2,1,0:T(2,128)(2,1)S(1)} %get-tuple-element.15.finished, bf16[8,8,8,2,256]{4,3,2,1,0:T(2,128)(2,1)S(1)} %get-tuple-element.16.returned, ...), custom_call_target="tpu_custom_call" | custom-call | bytes 3145728 | tf_op jit(solution)/shard_map/pallas_call | solution.py:575
Async XLA Ops:
  0.0 0.7 %copy-start.6 = (s32[6,32]{1,0:T(8,128)S(1)}, s32[6,32]{1,0:T(8,128)}, u32[]{:S(2)}) copy-start(s32[6,32]{1,0:T(8,128)} %mask.3) | copy-start | bytes 2308
  0.7 1.4 %copy-start = (bf16[48,32,2,256]{3,2,1,0:T(2,128)(2,1)S(1)}, bf16[48,32,2,256]{3,2,1,0:T(2,128)(2,1)}, u32[]{:S(2)}) copy-start(bf16[48,32,2,256]{3,2,1,0:T(2,128)(2,1)} %fields.1) | copy-start | bytes 4718596
  0.7 1.5 %copy-start.1 = (bf16[256,1024]{1,0:T(8,128)(2,1)S(1)}, bf16[256,1024]{1,0:T(8,128)(2,1)}, u32[]{:S(2)}) copy-start(bf16[256,1024]{1,0:T(8,128)(2,1)} %w_up.1) | copy-start | bytes 1572868
  0.7 1.7 %copy-start.2 = (bf16[1024,256]{1,0:T(8,128)(2,1)S(1)}, bf16[1024,256]{1,0:T(8,128)(2,1)}, u32[]{:S(2)}) copy-start(bf16[1024,256]{1,0:T(8,128)(2,1)} %w_down.1) | copy-start | bytes 1572868
  0.7 1.8 %copy-start.3 = (bf16[256,768]{1,0:T(8,128)(2,1)S(1)}, bf16[256,768]{1,0:T(8,128)(2,1)}, u32[]{:S(2)}) copy-start(bf16[256,768]{1,0:T(8,128)(2,1)} %w_qkv.1) | copy-start | bytes 1179652
  0.7 1.8 %copy-start.4 = (bf16[256,256]{1,0:T(8,128)(2,1)S(1)}, bf16[256,256]{1,0:T(8,128)(2,1)}, u32[]{:S(2)}) copy-start(bf16[256,256]{1,0:T(8,128)(2,1)} %w_proj.1) | copy-start | bytes 393220
  0.7 1.8 %copy-start.5 = (f32[8,675]{1,0:T(8,128)S(1)}, f32[8,675]{1,0:T(8,128)}, u32[]{:S(2)}) copy-start(f32[8,675]{1,0:T(8,128)} %rel_bias.1) | copy-start | bytes 64804
  0.7 1.8 %copy-start.8 = (f32[256]{0:T(256)S(1)}, f32[256]{0:T(256)}, u32[]{:S(2)}) copy-start(f32[256]{0:T(256)} %param.11) | copy-start | bytes 3076
  0.7 1.8 %copy-start.9 = (f32[256]{0:T(256)S(1)}, f32[256]{0:T(256)}, u32[]{:S(2)}) copy-start(f32[256]{0:T(256)} %param.15) | copy-start | bytes 3076
  2.5 20.1 %copy-start.7 = (s32[6,32]{1,0:T(8,128)S(1)}, s32[6,32]{1,0:T(8,128)}, u32[]{:S(2)}) copy-start(s32[6,32]{1,0:T(8,128)} %mask.3) | copy-start | bytes 2308

commit v2 on v1

v2 whole, which is shorter than its diff:
```python
import functools
import math

import jax
import jax.numpy as jnp
from jax import lax
from jax.experimental import pallas as pl
from jax.experimental.pallas import tpu as pltpu
from jax.sharding import PartitionSpec as P

WIN_LAT = 8
WIN_LON = 8
NORM_FLOOR = 0.25
MESH = pl.DeviceIdType.MESH
LOG2E = math.log2(math.e)
ROOT_HALF = math.sqrt(0.5)
PAIR = 2
EARLY_PAIRS = 2
LEAVING_PAIRS = 3


def dot(left, right):
    return jnp.dot(left, right, preferred_element_type=jnp.float32)


def normalise(values, gain):
    share = 1.0 / values.shape[0]
    average = jnp.sum(values, axis=0, keepdims=True) * share
    centred = values - average
    spread = jnp.sum(centred * centred, axis=0, keepdims=True) * share
    return (centred * lax.rsqrt(spread + NORM_FLOOR) * gain).astype(jnp.bfloat16)


def wide(gain, columns):
    return jnp.concatenate([gain] * (columns // gain.shape[1]), axis=1)


def flip_steps(store, blocks, weights):
    flipped = jnp.concatenate([block.T for block in blocks], axis=1)
    gain = wide(weights["gain_one"][...], flipped.shape[1])
    store.extend([flipped, normalise(flipped.astype(jnp.float32), gain)])
    yield


def attention_steps(store, flipped, normed, weights):
    qkv_t, proj_t, bias = weights["qkv"], weights["proj"], weights["bias"]
    features, columns = normed.shape
    half, tokens, _ = bias.shape
    dim = features // (2 * half)
    scale = LOG2E / math.sqrt(dim)
    key_t = dot(qkv_t[features : 2 * features], normed).astype(jnp.bfloat16)
    yield
    query_t = (dot(qkv_t[:features], normed) * scale).astype(jnp.bfloat16)
    yield
    value_t = dot(qkv_t[2 * features :], normed).astype(jnp.bfloat16)
    yield
    lane_head = lax.broadcasted_iota(jnp.int32, (tokens, features), 1) // dim % half
    nothing = jnp.zeros((features // 2, tokens), jnp.bfloat16)
    ones = jnp.ones((16, tokens), jnp.bfloat16)
    spans = [slice(n, n + tokens) for n in range(0, columns, tokens)]
    every = []
    for lanes in spans:
        key = key_t[:, lanes].T
        masked = [jnp.where(lane_head == h, key, jnp.zeros_like(key)) for h in range(half)]
        upper = jnp.concatenate([query_t[: features // 2, lanes], nothing], axis=1)
        lower = jnp.concatenate([nothing, query_t[features // 2 :, lanes]], axis=1)
        every.append(dot(jnp.concatenate(masked, axis=0), jnp.concatenate([upper, lower], axis=0)))
        yield
    mixed = []
    for lanes, products in zip(spans, every):
        first, second = [], []
        for h in range(half):
            scores = products[h * tokens : (h + 1) * tokens] + bias[h]
            power = jnp.exp2(scores - jnp.max(scores, axis=0, keepdims=True)).astype(jnp.bfloat16)
            one, two = h * dim, (h + half) * dim
            rows = [value_t[one : one + dim, lanes], value_t[two : two + dim, lanes], ones]
            piece = dot(jnp.concatenate(rows, axis=0), power)
            share = 1.0 / piece[2 * dim : 2 * dim + 1]
            first.append((piece[:dim, :tokens] * share[:, :tokens]).astype(jnp.bfloat16))
            second.append((piece[dim : 2 * dim, tokens:] * share[:, tokens:]).astype(jnp.bfloat16))
            yield
        mixed.append(jnp.concatenate(first + second, axis=0))
    projected = dot(proj_t[...], jnp.concatenate(mixed, axis=1))
    store.append((flipped.astype(jnp.float32) + projected).astype(jnp.bfloat16))
    yield


def mlp_steps(store, middle, weights, tokens):
    up_t, down_t, gain = weights["up"], weights["down"], weights["gain_two"]
    features, hidden = middle.shape[0], up_t.shape[0]
    residual = middle.astype(jnp.float32)
    normed = normalise(residual, wide(gain[...], middle.shape[1]))
    yield
    total = None
    for part in range(hidden // features):
        rows = slice(part * features, (part + 1) * features)
        grown = dot(up_t[rows], normed)
        yield
        grown = (grown * (1.0 + lax.erf(grown))).astype(jnp.bfloat16)
        piece = dot(down_t[:, rows], grown)
        total = piece if total is None else total + piece
        yield
    result = (residual + total * ROOT_HALF).astype(jnp.bfloat16)
    for n in range(middle.shape[1] // tokens):
        store.append(result[:, n * tokens : (n + 1) * tokens].T)
    yield


def weave(*steps):
    steps = list(steps)
    while steps:
        for chain in list(steps):
            try:
                next(chain)
            except StopIteration:
                steps.remove(chain)


def bias_strips(rel_bias, padded, strips, levels):
    heads, length = rel_bias.shape
    col_step = 2 * levels - 1
    row_step = (2 * WIN_LON - 1) * col_step
    offsets = [c * col_step + lev for c in range(WIN_LON) for lev in range(levels)]
    top = offsets[-1]
    width = padded.shape[1] - 128
    padded[...] = jnp.zeros_like(padded)
    padded[:, :length] = rel_bias[...] * LOG2E
    table = padded[...]
    left = jnp.concatenate([table[:, top - q : top - q + width] for q in offsets], axis=0)
    group = WIN_LON * levels
    lane = lax.broadcasted_iota(jnp.int32, (width, strips.shape[2]), 1)
    inner = lane % group
    target = lane // group * row_step + inner // levels * col_step + inner % levels
    pick = lax.broadcasted_iota(jnp.int32, target.shape, 0) == target
    found = jnp.dot(
        left,
        pick.astype(jnp.float32),
        precision=lax.Precision.HIGHEST,
        preferred_element_type=jnp.float32,
    )
    for place in range(group):
        strips[:, place, :] = found[place * heads : (place + 1) * heads]


def bias_table(strips, bias):
    heads, group, _ = strips.shape
    tokens = WIN_LAT * group
    for row in range(WIN_LAT):
        first = (WIN_LAT - 1 - row) * group
        piece = strips[:, :, first : first + tokens]
        places = slice(row * group, (row + 1) * group)
        bias[:, places, :tokens] = piece[: heads // 2]
        bias[:, places, tokens:] = piece[heads // 2 :]


class Sizes:
    def __init__(self, fields_shape):
        self.rows = fields_shape[0] // WIN_LAT
        self.cols = fields_shape[1] // WIN_LON
        self.count = self.rows * self.cols
        self.late = -(-((self.rows - 1) * self.cols // 2) // PAIR) * PAIR
        self.early = EARLY_PAIRS * PAIR
        self.leaving = min(LEAVING_PAIRS * PAIR, self.late)
        self.edge = self.rows + self.cols - 1

    def interior(self, window):
        return window // self.cols < self.rows - 1 and window % self.cols < self.cols - 1


def share_out(sizes, mask, device):
    def tally(d):
        inside, outside = jnp.int32(0), jnp.int32(0)
        for window in range(sizes.count):
            ocean = mask[window // sizes.cols, d * sizes.cols + window % sizes.cols]
            if sizes.interior(window):
                inside = inside + ocean
            else:
                outside = outside + ocean
        return inside, outside

    last = lax.axis_size("lon") - 1

    def pass_on(d, carried):
        inside, outside = tally(d)
        early = jnp.minimum(inside, sizes.early)
        excess = carried + inside + outside - early - sizes.late
        leaving = jnp.minimum(jnp.minimum(excess, inside - early), sizes.leaving)
        return jnp.where(d == last, 0, jnp.maximum(leaving, 0))

    coming = lax.fori_loop(0, device, pass_on, jnp.int32(0))
    leaving = pass_on(device, coming)
    inside, outside = tally(device)
    return coming, leaving, jnp.minimum(inside, sizes.early), inside, outside


def first_kernel(token):
    token[...] = jnp.zeros_like(token)


def main_kernel(
    sizes,
    mask, token, fields, rel_bias, gain_one, w_qkv, w_proj, gain_two, w_up, w_down,
    results, codes, ext, qkv_t, proj_t, up_t, down_t, gain_one_t, gain_two_t, bias,
    arrived, leave, flipped, normed, middle, inner, outer, padded, strips,
    halo_send, halo_recv, out_send, out_recv, back_send, back_recv,
):
    lat_cells, lon_cells, levels, features = fields.shape
    lat_half, lon_half = WIN_LAT // 2, WIN_LON // 2
    tokens = WIN_LAT * WIN_LON * levels
    lat, lon = lax.axis_index("lat"), lax.axis_index("lon")
    lat_size, lon_size = lax.axis_size("lat"), lax.axis_size("lon")
    last = lon_size - 1
    west, east = (lon + lon_size - 1) % lon_size, (lon + 1) % lon_size
    barrier = pltpu.get_barrier_semaphore()

    def greet(row, col):
        pl.semaphore_signal(barrier, inc=1, device_id=(row, col), device_id_type=MESH)

    greet(lat, east)
    greet(lat, west)

    @pl.when(lat < lat_size - 1)
    def _():
        greet(lat + 1, lon)
        greet(lat + 1, east)

    def transfer(source, target, send, recv, row, col):
        return pltpu.make_async_remote_copy(
            src_ref=source, dst_ref=target, send_sem=send, recv_sem=recv,
            device_id=(row, col), device_id_type=MESH,
        )

    up = jnp.maximum(lat - 1, 0)
    below, beside = pl.ds(lat_cells, lat_half), pl.ds(lon_cells, lon_half)
    rows, cols = pl.ds(lat_half, lat_cells - lat_half), pl.ds(lon_half, lon_cells - lon_half)
    top, left = pl.ds(0, lat_half), pl.ds(0, lon_half)
    to_north = transfer(
        fields.at[top, cols], ext.at[below, cols], halo_send.at[0], halo_recv.at[0], up, lon
    )
    to_west = transfer(
        fields.at[rows, left], ext.at[rows, beside], halo_send.at[1], halo_recv.at[1], lat, west
    )
    to_corner = transfer(
        fields.at[top, left], ext.at[below, beside], halo_send.at[2], halo_recv.at[2], up, west
    )

    @pl.when(lat > 0)
    def _():
        pl.semaphore_wait(barrier, 4)
        to_north.start()
        to_corner.start()

    @pl.when(lat == 0)
    def _():
        pl.semaphore_wait(barrier, 2)

    to_west.start()
    coming, going, early, _, edges = share_out(sizes, mask, lon)
    first_col = lon * sizes.cols
    for chain, inside_only in ((inner, True), (outer, False)):
        following = jnp.int32(sizes.count)
        chain[0, sizes.count] = following
        chain[0, sizes.count + 1] = following
        for window in reversed(range(sizes.count)):
            if sizes.interior(window) == inside_only:
                ocean = mask[window // sizes.cols, first_col + window % sizes.cols]
                following = jnp.where(ocean == 1, window, following)
            chain[0, window] = following
        spot = following
        for n in range(sizes.count):
            chain[1, n] = jnp.where(spot == sizes.count, 0, spot)
            spot = chain[0, spot + 1]

    def fetch(source, window):
        row, col = window // sizes.cols, window % sizes.cols
        row_cells = pl.ds(row * WIN_LAT + lat_half, WIN_LAT)
        return source[row_cells, pl.ds(col * WIN_LON + lon_half, WIN_LON)]

    def outward(slot):
        return transfer(
            leave.at[slot], arrived.at[slot], out_send.at[slot], out_recv.at[slot],
            lat, jnp.minimum(lon + 1, last),
        )

    def homeward(pair):
        slots = pl.ds(sizes.early + sizes.late + pair * PAIR, PAIR)
        return transfer(
            results.at[pl.ds(sizes.early + pair * PAIR, PAIR)], results.at[slots],
            back_send.at[pair], back_recv.at[pair], lat, jnp.maximum(lon - 1, 0),
        )

    def pack(slot, carry):
        leave[slot] = fetch(fields, inner[1, sizes.early + slot])

        @pl.when(lon < last)
        def _():
            outward(slot).start()

        return carry

    lax.fori_loop(0, sizes.leaving, pack, 0)
    bias_strips(rel_bias, padded, strips, levels)
    bias_table(strips, bias)
    gain_one_t[...] = jnp.broadcast_to(gain_one[...], (128, features)).T
    gain_two_t[...] = jnp.broadcast_to(gain_two[...] * ROOT_HALF, (128, features)).T
    for source, target in ((w_qkv, qkv_t), (w_proj, proj_t), (w_up, up_t), (w_down, down_t)):
        target[...] = source[...].T
    weights = dict(
        qkv=qkv_t, proj=proj_t, up=up_t, down=down_t,
        gain_one=gain_one_t, gain_two=gain_two_t, bias=bias,
    )
    early_pairs, late_pairs, leaving_pairs = (
        sizes.early // PAIR, sizes.late // PAIR, sizes.leaving // PAIR
    )

    def early_blocks(step):
        windows = [fetch(fields, inner[1, step * PAIR + n]) for n in range(PAIR)]
        return [window.reshape(tokens, features) for window in windows]

    def late_blocks(pair):
        blocks = []
        for n in range(PAIR):
            slot = pair * PAIR + n
            rank = slot - coming
            edge = jnp.clip(rank, 0, sizes.count - 1)
            other = jnp.clip(early + going + rank - edges, 0, sizes.count - 1)
            mine = fetch(ext, jnp.where(rank < edges, outer[1, edge], inner[1, other]))
            sent = arrived[jnp.minimum(slot, sizes.leaving - 1)]
            block = jnp.where(rank >= 0, mine, sent)
            blocks.append(block.reshape(tokens, features))
        return blocks

    def put(step, flip):
        flipped[step % 2], normed[step % 2] = flip

    def keep(step, windows):
        for n, window in enumerate(windows):
            results[step * PAIR + n] = window.reshape(results.shape[1:])

    def advance(step, before=True, blocks=None):
        new, windows, flip = [], [], []
        chains = [attention_steps(new, flipped[step % 2], normed[step % 2], weights)]
        if before:
            chains.insert(0, mlp_steps(windows, middle[(step + 1) % 2], weights, tokens))
        weave(*chains)
        if blocks is not None:
            weave(flip_steps(flip, blocks, weights))
            put(step + 1, flip)
        if before:
            keep(step - 1, windows)
        middle[step % 2] = new[0]

    def prepare(step, blocks):
        flip = []
        weave(flip_steps(flip, blocks, weights))
        put(step, flip)

    prepare(0, early_blocks(0))
    advance(0, before=False, blocks=early_blocks(1) if early_pairs > 1 else None)

    def early_step(step, carry):
        advance(step, blocks=early_blocks(step + 1))
        return carry

    lax.fori_loop(1, early_pairs - 1, early_step, 0)
    if early_pairs > 1:
        advance(early_pairs - 1)
    inside_rows, inside_cols = pl.ds(lat_half, lat_cells - lat_half), pl.ds(lon_half, lon_cells - lon_half)
    ext[inside_rows, inside_cols] = fields[inside_rows, inside_cols]
    to_west.wait_recv()

    @pl.when(lat < lat_size - 1)
    def _():
        to_north.wait_recv()
        to_corner.wait_recv()

    def receive(pair):
        @pl.when((pair < leaving_pairs) & (lon > 0))
        def _():
            for n in range(PAIR):
                outward(pair * PAIR + n).wait_recv()

    def send_home(pair):
        @pl.when((pair >= 0) & (pair < leaving_pairs) & (lon > 0))
        def _():
            homeward(pair).start()

    receive(jnp.int32(0))
    prepare(early_pairs, late_blocks(0))

    def late_step(pair, carry):
        receive(pair + 1)
        advance(early_pairs + pair, blocks=late_blocks(jnp.minimum(pair + 1, late_pairs - 1)))
        send_home(pair - 1)
        return carry

    lax.fori_loop(0, late_pairs, late_step, 0)
    steps = early_pairs + late_pairs
    windows = []
    weave(mlp_steps(windows, middle[(steps - 1) % 2], weights, tokens))
    keep(steps - 1, windows)
    if late_pairs <= leaving_pairs:
        send_home(jnp.int32(late_pairs - 1))

    room = sizes.late - coming
    back = sizes.early + sizes.late
    results[back + sizes.leaving] = jnp.zeros(results.shape[1:], results.dtype)
    inside_rank, edge_rank = jnp.int32(0), jnp.int32(0)
    for window in range(sizes.count):
        ocean = mask[window // sizes.cols, first_col + window % sizes.cols]
        if sizes.interior(window):
            rank = edges + inside_rank - early - going
        else:
            rank = edge_rank
        code = jnp.where(rank < room, sizes.early + coming + rank, -1)
        if sizes.interior(window):
            code = jnp.where(inside_rank < early + going, back + inside_rank - early, code)
            code = jnp.where(inside_rank < early, inside_rank, code)
            inside_rank = inside_rank + ocean
        else:
            edge_rank = edge_rank + ocean
        codes[window] = jnp.where(ocean == 1, code, back + sizes.leaving)

    to_west.wait_send()

    @pl.when(lat > 0)
    def _():
        to_north.wait_send()
        to_corner.wait_send()

    @pl.when(lon > 0)
    def _():
        for pair in range(leaving_pairs):
            homeward(pair).wait_send()

    @pl.when(lon < last)
    def _():
        for slot in range(sizes.leaving):
            outward(slot).wait_send()
        for pair in range(leaving_pairs):
            homeward(pair).wait_recv()


def place_kernel(
    sizes,
    codes, results, ext, qkv_t, proj_t, up_t, down_t, gain_one_t, gain_two_t, bias,
    output, extra, sems,
):
    lat_half, lon_half = WIN_LAT // 2, WIN_LON // 2
    nothing = results.shape[0] - 1

    def spot(window):
        row, col = window // sizes.cols, window % sizes.cols
        return output.at[pl.ds(row * WIN_LAT, WIN_LAT), pl.ds(col * WIN_LON, WIN_LON)]

    lost = jnp.int32(0)
    for window in range(sizes.count):
        code = codes[window]
        lost = jnp.minimum(lost, code)
        source = results.at[jnp.where(code < 0, nothing, code)]
        pltpu.make_async_copy(source, spot(window), sems.at[window]).start()
    for window in range(sizes.count):
        pltpu.make_async_copy(results.at[nothing], spot(window), sems.at[window]).wait()

    @pl.when(lost < 0)
    def _():
        def again(window, carry):
            @pl.when(codes[window] < 0)
            def _():
                row, col = window // sizes.cols, window % sizes.cols
                row_cells = pl.ds(row * WIN_LAT + lat_half, WIN_LAT)
                block = ext[row_cells, pl.ds(col * WIN_LON + lon_half, WIN_LON)]
                weights = dict(
                    qkv=qkv_t, proj=proj_t, up=up_t, down=down_t,
                    gain_one=gain_one_t, gain_two=gain_two_t, bias=bias,
                )
                tokens = block.shape[0] * block.shape[1] * block.shape[2]
                flip, middle, windows = [], [], []
                weave(flip_steps(flip, [block.reshape(tokens, block.shape[3])], weights))
                weave(attention_steps(middle, flip[0], flip[1], weights))
                weave(mlp_steps(windows, middle[0], weights, tokens))
                extra[...] = windows[0].reshape(extra.shape)
                copy = pltpu.make_async_copy(extra, spot(window), sems.at[window])
                copy.start()
                copy.wait()

            return carry

        lax.fori_loop(0, sizes.count, again, 0)


def vmem():
    return pl.BlockSpec(memory_space=pltpu.VMEM)


def smem():
    return pl.BlockSpec(memory_space=pltpu.SMEM)


def any_space():
    return pl.BlockSpec(memory_space=pl.ANY)


def cost(flops, moved):
    return pl.CostEstimate(flops=flops, bytes_accessed=moved, transcendentals=0)


def body(fields, ocean_mask, gain_one, w_qkv, rel_bias, w_proj, gain_two, w_up, w_down):
    sizes = Sizes(fields.shape)
    lat_cells, lon_cells, levels, features = fields.shape
    heads, length = rel_bias.shape
    group = WIN_LON * levels
    tokens = WIN_LAT * group
    window = (WIN_LAT, WIN_LON, levels, features)
    bf16, f32 = jnp.bfloat16, jnp.float32
    shape = jax.ShapeDtypeStruct
    gains = [gain_one.reshape(1, -1), gain_two.reshape(1, -1)]
    sources = [w_qkv, w_proj, w_up, w_down]
    flips = [shape(w.shape[::-1], w.dtype) for w in sources]
    dma = pltpu.SemaphoreType.DMA
    pairs = sizes.leaving // PAIR
    token = pl.pallas_call(
        first_kernel,
        out_shape=shape((8, 128), f32),
        out_specs=vmem(),
        cost_estimate=cost(2**36, 2**26),
        compiler_params=pltpu.CompilerParams(vmem_limit_bytes=2**20),
    )()
    pair_shape = (2, features, PAIR * tokens)
    outcome = pl.pallas_call(
        functools.partial(main_kernel, sizes),
        out_shape=[
            shape((sizes.early + sizes.late + sizes.leaving + 1,) + window, bf16),
            shape((sizes.count,), jnp.int32),
            shape((lat_cells + WIN_LAT // 2, lon_cells + WIN_LON // 2, levels, features), bf16),
        ]
        + flips
        + [shape((features, 128), f32)] * 2
        + [shape((heads // 2, tokens, 2 * tokens), f32)],
        in_specs=[smem()] + [vmem()] * 9,
        out_specs=[vmem(), smem()] + [vmem()] * 8,
        scratch_shapes=[
            pltpu.VMEM((sizes.leaving,) + window, bf16),
            pltpu.VMEM((sizes.leaving,) + window, bf16),
            pltpu.VMEM(pair_shape, bf16),
            pltpu.VMEM(pair_shape, bf16),
            pltpu.VMEM(pair_shape, bf16),
            pltpu.SMEM((2, sizes.count + 2), jnp.int32),
            pltpu.SMEM((2, sizes.count + 2), jnp.int32),
            pltpu.VMEM((heads, (length + 255) // 128 * 128), f32),
            pltpu.VMEM((heads, group, 2 * tokens), f32),
        ]
        + [dma((3,)), dma((3,)), dma((sizes.leaving,)), dma((sizes.leaving,))]
        + [dma((pairs,)), dma((pairs,))],
        cost_estimate=cost(0, fields.size),
        compiler_params=pltpu.CompilerParams(
            collective_id=0, has_side_effects=True, vmem_limit_bytes=24 * 2**20
        ),
    )(ocean_mask, token, fields, rel_bias, gains[0], w_qkv, w_proj, gains[1], w_up, w_down)
    results, codes = outcome[:2]
    return pl.pallas_call(
        functools.partial(place_kernel, sizes),
        out_shape=shape(fields.shape, fields.dtype),
        in_specs=[smem()] + [vmem()] * 9,
        out_specs=any_space(),
        scratch_shapes=[pltpu.VMEM(window, bf16), dma((sizes.count,))],
        cost_estimate=cost(0, 4 * fields.size),
        compiler_params=pltpu.CompilerParams(vmem_limit_bytes=12 * 2**20),
    )(codes, results, *outcome[2:])


def solution(mesh):
    in_specs = (P("lat", "lon", None, None), P("lat", None), P(), P(), P(), P(), P(), P(), P())
    out_specs = P("lat", "lon", None, None)
    return jax.shard_map(body, mesh=mesh, in_specs=in_specs, out_specs=out_specs, check_vma=False)
```

time: 25.1 us -> 23.9 us (0.952)
  Pallas kernels: 23.7 us -> 21.9 us
  local copies, waits for them, and re-layouts: 1.15 us -> 1.78 us
    pallas_call x1, Pallas kernels: 1.34 us -> 0.01 us  [body(): pl.pallas_call(first_kernel, out_shape=shape((8, 128), f32), out_specs=vm...]
    unnamed x20 -> x18, local copies, waits for them, and re-layouts: 1.15 us -> 1.78 us
    pallas_call x1, Pallas kernels: 2.25 us -> 1.88 us  [body(): pl.pallas_call(functools.partial(place_kernel, sizes), out_shape=shape(fi...]
where the time goes in v2:
time: 23.9 us; the launch traced here: 23.7 us
  Pallas kernels  21.9 us (92%)
  local copies, waits for them, and re-layouts  1.78 us (7%)
    pallas_call x1, Pallas kernels, body(): pl.pallas_call(functools.partial(main_kernel, sizes), out_shape=[shape((s...  20 us
    pallas_call x1, Pallas kernels, body(): pl.pallas_call(functools.partial(place_kernel, sizes), out_shape=shape(fi...  1.88 us
    unnamed x18, local copies, waits for them, and re-layouts  1.78 us

profile of v2, /device:TPU:1, one launch (start us, length us, event | category | flops | bytes accessed | tf_op | source)
XLA Modules:
  0.0 23.7 jit_solution(7524096611721627069)
XLA Ops:
  0.0 0.0 copy-start
  0.0 0.0 copy-start.1
  0.0 0.0 copy-start.2
  0.0 0.0 copy-start.3
  0.0 0.0 copy-start.4
  0.0 0.0 copy-start.5
  0.0 0.0 copy-start.6
  0.0 0.0 copy-start.7
  0.1 0.0 copy-start.8
  0.1 1.3 %copy-done = bf16[48,32,2,256]{3,2,1,0:T(2,128)(2,1)S(1)} copy-done((bf16[48,32,2,256]{3,2,1,0:T(2,128)(2,1)S(1)}, bf16[48,32,2,256]{3,2,1,0:T(2,128)(2,1)}, u32[]{:S(2)}) %copy-start) | copy-done | bytes 1572888
  1.4 0.1 copy-done.1
  1.5 0.2 copy-done.2
  1.7 0.1 copy-done.3
  1.8 0.0 copy-done.4
  1.8 0.0 copy-done.5
  1.8 0.0 copy-done.6
  1.8 0.0 copy-done.7
  1.8 0.0 copy-done.8
  1.8 20.0 %shard_map.92 = (bf16[21,8,8,2,256]{4,3,2,1,0:T(2,128)(2,1)S(1)}, s32[24]{0:T(128)S(1)}, bf16[52,36,2,256]{3,2,1,0:T(2,128)(2,1)S(1)}, bf16[768,256]{1,0:T(8,128...) custom-call(s32[6,32]{1,0:T(8,128)S(1)} %copy-done.6, ...), custom_call_target="tpu_custom_call" | custom-call | bytes 786432 | tf_op jit(solution)/shard_map/pallas_call | solution.py:530
  21.9 1.9 %shard_map.93 = bf16[48,32,2,256]{3,2,1,0:T(2,128)(2,1)} custom-call(s32[24]{0:T(128)S(1)} %get-tuple-element.15.codes, bf16[21,8,8,2,256]{4,3,2,1,0:T(2,128)(2,1)S(1)} %get-tuple-element.16.results, bf16[52,36,2,256]{3,2,1,0:T(2,128)(2,1)S(1)} %get-tuple-element.17.ext, bf16[768,256]{1,0:T(8,128)(2,1)S(1)} %get-tuple-element.18.qkv_t, ...), custom_call_target="tpu_custom_call" | custom-call | bytes 3145728 | tf_op jit(solution)/shard_map/pallas_call | solution.py:561
  (1 shorter events, 0.0 us)
Async XLA Ops:
  0.0 1.4 %copy-start = (bf16[48,32,2,256]{3,2,1,0:T(2,128)(2,1)S(1)}, bf16[48,32,2,256]{3,2,1,0:T(2,128)(2,1)}, u32[]{:S(2)}) copy-start(bf16[48,32,2,256]{3,2,1,0:T(2,128)(2,1)} %fields.1) | copy-start | bytes 4718596
  0.0 1.5 %copy-start.1 = (bf16[256,1024]{1,0:T(8,128)(2,1)S(1)}, bf16[256,1024]{1,0:T(8,128)(2,1)}, u32[]{:S(2)}) copy-start(bf16[256,1024]{1,0:T(8,128)(2,1)} %w_up.1) | copy-start | bytes 1572868
  0.0 1.7 %copy-start.2 = (bf16[1024,256]{1,0:T(8,128)(2,1)S(1)}, bf16[1024,256]{1,0:T(8,128)(2,1)}, u32[]{:S(2)}) copy-start(bf16[1024,256]{1,0:T(8,128)(2,1)} %w_down.1) | copy-start | bytes 1572868
  0.0 1.8 %copy-start.3 = (bf16[256,768]{1,0:T(8,128)(2,1)S(1)}, bf16[256,768]{1,0:T(8,128)(2,1)}, u32[]{:S(2)}) copy-start(bf16[256,768]{1,0:T(8,128)(2,1)} %w_qkv.1) | copy-start | bytes 1179652
  0.0 1.8 %copy-start.4 = (bf16[256,256]{1,0:T(8,128)(2,1)S(1)}, bf16[256,256]{1,0:T(8,128)(2,1)}, u32[]{:S(2)}) copy-start(bf16[256,256]{1,0:T(8,128)(2,1)} %w_proj.1) | copy-start | bytes 393220
  0.0 1.8 %copy-start.5 = (f32[8,675]{1,0:T(8,128)S(1)}, f32[8,675]{1,0:T(8,128)}, u32[]{:S(2)}) copy-start(f32[8,675]{1,0:T(8,128)} %rel_bias.1) | copy-start | bytes 64804
  0.0 1.8 %copy-start.6 = (s32[6,32]{1,0:T(8,128)S(1)}, s32[6,32]{1,0:T(8,128)}, u32[]{:S(2)}) copy-start(s32[6,32]{1,0:T(8,128)} %mask.1) | copy-start | bytes 2308
  0.0 1.8 %copy-start.7 = (f32[256]{0:T(256)S(1)}, f32[256]{0:T(256)}, u32[]{:S(2)}) copy-start(f32[256]{0:T(256)} %param.11) | copy-start | bytes 3076
  0.1 1.8 %copy-start.8 = (f32[256]{0:T(256)S(1)}, f32[256]{0:T(256)}, u32[]{:S(2)}) copy-start(f32[256]{0:T(256)} %param.15) | copy-start | bytes 3076

commit v3 on v2

--- a/solution.py
+++ b/solution.py
@@ -15,8 +15,8 @@
 LOG2E = math.log2(math.e)
 ROOT_HALF = math.sqrt(0.5)
 PAIR = 2
-EARLY_PAIRS = 2
-LEAVING_PAIRS = 3
+EARLY_PAIRS = 3
+LEAVING_PAIRS = 2
 
 
 def dot(left, right):
@@ -244,17 +244,6 @@
         fields.at[top, left], ext.at[below, beside], halo_send.at[2], halo_recv.at[2], up, west
     )
 
-    @pl.when(lat > 0)
-    def _():
-        pl.semaphore_wait(barrier, 4)
-        to_north.start()
-        to_corner.start()
-
-    @pl.when(lat == 0)
-    def _():
-        pl.semaphore_wait(barrier, 2)
-
-    to_west.start()
     coming, going, early, _, edges = share_out(sizes, mask, lon)
     first_col = lon * sizes.cols
     for chain, inside_only in ((inner, True), (outer, False)):
@@ -291,14 +280,27 @@
 
     def pack(slot, carry):
         leave[slot] = fetch(fields, inner[1, sizes.early + slot])
-
-        @pl.when(lon < last)
-        def _():
+        return carry
+
+    lax.fori_loop(0, sizes.leaving, pack, 0)
+
+    @pl.when(lat > 0)
+    def _():
+        pl.semaphore_wait(barrier, 4)
+        to_north.start()
+        to_corner.start()
+
+    @pl.when(lat == 0)
+    def _():
+        pl.semaphore_wait(barrier, 2)
+
+    to_west.start()
+
+    @pl.when(lon < last)
+    def _():
+        for slot in range(sizes.leaving):
             outward(slot).start()
 
-        return carry
-
-    lax.fori_loop(0, sizes.leaving, pack, 0)
     bias_strips(rel_bias, padded, strips, levels)
     bias_table(strips, bias)
     gain_one_t[...] = jnp.broadcast_to(gain_one[...], (128, features)).T

time: 23.9 us -> 21.8 us (0.912)
  the two profiles are of different devices: /device:TPU:1 before, /device:TPU:0 now
where the time goes in v3:
time: 21.8 us; the launch traced here: 21.7 us
  Pallas kernels  19.8 us (91%)
  local copies, waits for them, and re-layouts  1.79 us (8%)
    pallas_call x1, Pallas kernels, body(): pl.pallas_call(functools.partial(main_kernel, sizes), out_shape=[shape((s...  17.9 us
    pallas_call x1, Pallas kernels, body(): pl.pallas_call(functools.partial(place_kernel, sizes), out_shape=shape(fi...  1.88 us
    unnamed x18, local copies, waits for them, and re-layouts  1.79 us

profile of v3, /device:TPU:0, one launch (start us, length us, event | category | flops | bytes accessed | tf_op | source)
XLA Modules:
  0.0 21.7 jit_solution(12704932889534793078)
XLA Ops:
  0.0 0.0 copy-start
  0.0 0.0 copy-start.1
  0.0 0.0 copy-start.2
  0.0 0.0 copy-start.3
  0.0 0.0 copy-start.4
  0.0 0.0 copy-start.5
  0.0 0.0 copy-start.6
  0.0 0.0 copy-start.7
  0.0 0.0 copy-start.8
  0.1 1.3 %copy-done = bf16[48,32,2,256]{3,2,1,0:T(2,128)(2,1)S(1)} copy-done((bf16[48,32,2,256]{3,2,1,0:T(2,128)(2,1)S(1)}, bf16[48,32,2,256]{3,2,1,0:T(2,128)(2,1)}, u32[]{:S(2)}) %copy-start) | copy-done | bytes 1572888
  1.4 0.1 copy-done.1
  1.5 0.2 copy-done.2
  1.7 0.1 copy-done.3
  1.8 0.0 copy-done.4
  1.8 0.0 copy-done.5
  1.8 0.0 copy-done.6
  1.8 0.0 copy-done.7
  1.8 0.0 copy-done.8
  1.8 17.9 %shard_map.92 = (bf16[21,8,8,2,256]{4,3,2,1,0:T(2,128)(2,1)S(1)}, s32[24]{0:T(128)S(1)}, bf16[52,36,2,256]{3,2,1,0:T(2,128)(2,1)S(1)}, bf16[768,256]{1,0:T(8,128...) custom-call(s32[6,32]{1,0:T(8,128)S(1)} %copy-done.6, ...), custom_call_target="tpu_custom_call" | custom-call | bytes 786432 | tf_op jit(solution)/shard_map/pallas_call | solution.py:532
  19.8 1.9 %shard_map.93 = bf16[48,32,2,256]{3,2,1,0:T(2,128)(2,1)} custom-call(s32[24]{0:T(128)S(1)} %get-tuple-element.15.codes, bf16[21,8,8,2,256]{4,3,2,1,0:T(2,128)(2,1)S(1)} %get-tuple-element.16.results, bf16[52,36,2,256]{3,2,1,0:T(2,128)(2,1)S(1)} %get-tuple-element.17.ext, bf16[768,256]{1,0:T(8,128)(2,1)S(1)} %get-tuple-element.18.qkv_t, ...), custom_call_target="tpu_custom_call" | custom-call | bytes 3145728 | tf_op jit(solution)/shard_map/pallas_call | solution.py:563
  (1 shorter events, 0.0 us)
Async XLA Ops:
  0.0 1.4 %copy-start = (bf16[48,32,2,256]{3,2,1,0:T(2,128)(2,1)S(1)}, bf16[48,32,2,256]{3,2,1,0:T(2,128)(2,1)}, u32[]{:S(2)}) copy-start(bf16[48,32,2,256]{3,2,1,0:T(2,128)(2,1)} %fields.1) | copy-start | bytes 4718596
  0.0 1.5 %copy-start.1 = (bf16[256,1024]{1,0:T(8,128)(2,1)S(1)}, bf16[256,1024]{1,0:T(8,128)(2,1)}, u32[]{:S(2)}) copy-start(bf16[256,1024]{1,0:T(8,128)(2,1)} %w_up.1) | copy-start | bytes 1572868
  0.0 1.7 %copy-start.2 = (bf16[1024,256]{1,0:T(8,128)(2,1)S(1)}, bf16[1024,256]{1,0:T(8,128)(2,1)}, u32[]{:S(2)}) copy-start(bf16[1024,256]{1,0:T(8,128)(2,1)} %w_down.1) | copy-start | bytes 1572868
  0.0 1.8 %copy-start.3 = (bf16[256,768]{1,0:T(8,128)(2,1)S(1)}, bf16[256,768]{1,0:T(8,128)(2,1)}, u32[]{:S(2)}) copy-start(bf16[256,768]{1,0:T(8,128)(2,1)} %w_qkv.1) | copy-start | bytes 1179652
  0.0 1.8 %copy-start.4 = (bf16[256,256]{1,0:T(8,128)(2,1)S(1)}, bf16[256,256]{1,0:T(8,128)(2,1)}, u32[]{:S(2)}) copy-start(bf16[256,256]{1,0:T(8,128)(2,1)} %w_proj.1) | copy-start | bytes 393220
  0.0 1.8 %copy-start.5 = (f32[8,675]{1,0:T(8,128)S(1)}, f32[8,675]{1,0:T(8,128)}, u32[]{:S(2)}) copy-start(f32[8,675]{1,0:T(8,128)} %rel_bias.1) | copy-start | bytes 64804
  0.0 1.8 %copy-start.6 = (s32[6,32]{1,0:T(8,128)S(1)}, s32[6,32]{1,0:T(8,128)}, u32[]{:S(2)}) copy-start(s32[6,32]{1,0:T(8,128)} %mask.1) | copy-start | bytes 2308
  0.0 1.8 %copy-start.7 = (f32[256]{0:T(256)S(1)}, f32[256]{0:T(256)}, u32[]{:S(2)}) copy-start(f32[256]{0:T(256)} %param.11) | copy-start | bytes 3076
  0.0 1.8 %copy-start.8 = (f32[256]{0:T(256)S(1)}, f32[256]{0:T(256)}, u32[]{:S(2)}) copy-start(f32[256]{0:T(256)} %param.15) | copy-start | bytes 3076
